TPU v7x, 32 devices: a whole 2x2x4 slice. The times are simulated.
32 devices in a mesh: dp: 2 (over y), ctx: 8 (over z, x), tp: 2 (over core).
Axes of the slice: x: 2, y: 2, z: 4, core: 2. Of those that a mesh axis runs over, the one named last changes fastest.
Arguments:
- queries: bfloat16 [4, 1024, 4096], P('dp', 'ctx', 'tp'), may hold values from -6 to 6
- keys: bfloat16 [4, 1024, 512], P('dp', 'ctx', 'tp'), may hold values from -6 to 6
- values: bfloat16 [4, 1024, 512], P('dp', 'ctx', 'tp'), may hold values from -6 to 6
- output_gradient: bfloat16 [4, 1024, 4096], P('dp', 'ctx', 'tp'), may hold values from -6 to 6
- sinks: float32 [64], P('tp'), may hold values from -1 to 3
- doc_starts: int32 [4, 64], P('dp'), may hold values from 0 to 2048, as said below
- valid_counts: int32 [4, 8], P('dp'), may hold values from 64 to 128
Outputs:
- query_grad: bfloat16 [4, 1024, 4096], P('dp', 'ctx', 'tp')
- key_grad: bfloat16 [4, 1024, 512], P('dp', 'ctx', 'tp')
- value_grad: bfloat16 [4, 1024, 512], P('dp', 'ctx', 'tp')
- sink_grad: float32 [64], P('tp')
Inputs may be any that keep to these rules, and one draw needn't show every extreme that they name: `doc_starts`: each row is strictly increasing, begins with 0 and ends with 2048; a start at or past 1024 opens no document.
All inputs are finite; a program needn't handle non-finite values.
Results may differ from a plain program's by a relative error of at most 0.0093.
Values may be sent and summed in bfloat16 or wider, within the bound.
A program may use at most 64 MiB of HBM per device.

v0:
```python
import math

import jax
import jax.numpy as jnp
from jax import lax
from jax.sharding import PartitionSpec as P

HEAD_DIMENSION = 64
WINDOW_LENGTH = 128


masked_score = -1e30


def passed_along(value, axis, steps):
    count = lax.axis_size(axis)
    first, last = (max(0, -steps), min(count, count - steps))
    return lax.ppermute(value, axis, [(source, source + steps) for source in range(first, last)])


def document_ids(starts, positions):
    return jnp.sum((starts[None, :] <= positions[:, None]).astype(jnp.int32), axis=1)


def key_valid_mask(counts, positions, block_rows):
    block_index = positions // block_rows
    offset = positions - block_index * block_rows
    matches = jnp.arange(counts.shape[0], dtype=jnp.int32)[None, :] == block_index[:, None]
    limits = jnp.sum(jnp.where(matches, counts[None, :], 0), axis=1)
    return offset < limits


def band_grads(
    query_tile_block,
    key_tile_block,
    value_tile_block,
    output_grad_block,
    query_pos,
    key_pos,
    query_doc,
    key_doc,
    key_valid,
    sink_logits,
):
    heads_kv = key_tile_block.shape[2]
    query_group_width = query_tile_block.shape[3]
    scaling = query_tile_block.shape[4] ** (-0.5)
    scores = (
        jnp.einsum(
            "nqhgd,nkhd->nhgqk",
            query_tile_block,
            key_tile_block,
            preferred_element_type=jnp.float32,
        )
        * scaling
    )
    allowed = (key_pos[:, None, :] <= query_pos[:, :, None]) & (
        query_pos[:, :, None] - key_pos[:, None, :] < WINDOW_LENGTH
    )
    allowed = allowed & (query_doc[:, :, None] == key_doc[:, None, :]) & key_valid[:, None, :]
    scores = jnp.where(allowed[:, None, None], scores, masked_score)
    sink_term = sink_logits.reshape(heads_kv, query_group_width)[None, :, :, None]
    maxima = jnp.maximum(jnp.max(scores, axis=-1), sink_term)
    powers = jnp.exp(scores - maxima[..., None])
    sink_exp = jnp.exp(sink_term - maxima)
    denominator = jnp.sum(powers, axis=-1) + sink_exp
    attend = powers / denominator[..., None]
    attend_low = attend.astype(jnp.bfloat16)
    context = jnp.einsum(
        "nhgqk,nkhd->nhgqd", attend_low, value_tile_block, preferred_element_type=jnp.float32
    )
    deltas = jnp.sum(
        jnp.transpose(output_grad_block, (0, 2, 3, 1, 4)).astype(jnp.float32) * context, axis=-1
    )
    grad_attend = jnp.einsum(
        "nqhgd,nkhd->nhgqk", output_grad_block, value_tile_block, preferred_element_type=jnp.float32
    )
    grad_score = attend * (grad_attend - deltas[..., None])
    score_low = grad_score.astype(jnp.bfloat16)
    query_grad = (
        jnp.einsum(
            "nhgqk,nkhd->nqhgd", score_low, key_tile_block, preferred_element_type=jnp.float32
        )
        * scaling
    )
    key_grad = (
        jnp.einsum(
            "nhgqk,nqhgd->nkhd", score_low, query_tile_block, preferred_element_type=jnp.float32
        )
        * scaling
    )
    value_grad = jnp.einsum(
        "nhgqk,nqhgd->nkhd", attend_low, output_grad_block, preferred_element_type=jnp.float32
    )
    sink_grad = -jnp.sum(sink_exp / denominator * deltas, axis=-1)
    return (
        query_grad,
        key_grad,
        value_grad,
        sink_grad.reshape(sink_grad.shape[0], heads_kv * query_group_width),
    )


def blockwise(entries, sink_logits):
    count_all = entries[0].shape[0]
    group_blocks = math.gcd(count_all, max(1, 512 // WINDOW_LENGTH))
    grouped = tuple(
        (
            member.reshape((count_all // group_blocks, group_blocks) + member.shape[1:])
            for member in entries
        )
    )

    def per_group(parts):
        return band_grads(*parts, sink_logits)

    results = lax.map(per_group, grouped)
    return tuple((member.reshape((count_all,) + member.shape[2:]) for member in results))


def block_facts(query_pos, key_pos, doc_starts, valid_counts, block_rows):
    collected = ([], [], [], [], [])
    for sequence_index in range(doc_starts.shape[0]):
        collected[0].append(query_pos)
        collected[1].append(key_pos)
        collected[2].append(
            document_ids(doc_starts[sequence_index], query_pos.reshape(-1)).reshape(query_pos.shape)
        )
        collected[3].append(
            document_ids(doc_starts[sequence_index], key_pos.reshape(-1)).reshape(key_pos.shape)
        )
        collected[4].append(
            key_valid_mask(valid_counts[sequence_index], key_pos.reshape(-1), block_rows).reshape(
                key_pos.shape
            )
        )
    return [jnp.concatenate(member, axis=0) for member in collected]


def local(queries, keys, values, output_gradient, sinks, doc_starts, valid_counts):
    seq_count, row_count, query_width = queries.shape
    kv_width = keys.shape[2]
    heads_kv = kv_width // HEAD_DIMENSION
    query_group_width = sinks.shape[0] // heads_kv
    block_tiles = row_count // WINDOW_LENGTH
    start_pos = lax.axis_index("ctx") * row_count
    halo_tails = passed_along((keys, values), "ctx", 1)

    def pair_rows(extended):
        shaped = extended.reshape(
            seq_count, block_tiles + 1, WINDOW_LENGTH, heads_kv, HEAD_DIMENSION
        )
        joined = jnp.concatenate([shaped[:, :-1], shaped[:, 1:]], axis=2)
        return joined.reshape(seq_count * block_tiles, 2 * WINDOW_LENGTH, heads_kv, HEAD_DIMENSION)

    query_lines = start_pos + jnp.arange(row_count, dtype=jnp.int32).reshape(
        block_tiles, WINDOW_LENGTH
    )
    key_lines = (
        start_pos - WINDOW_LENGTH + jnp.arange(row_count + WINDOW_LENGTH, dtype=jnp.int32)
    ).reshape(block_tiles + 1, WINDOW_LENGTH)
    key_lines = jnp.concatenate([key_lines[:-1], key_lines[1:]], axis=1)
    entries = [
        queries.reshape(
            seq_count * block_tiles, WINDOW_LENGTH, heads_kv, query_group_width, HEAD_DIMENSION
        ),
        pair_rows(jnp.concatenate([halo_tails[0], keys], axis=1)),
        pair_rows(jnp.concatenate([halo_tails[1], values], axis=1)),
        output_gradient.reshape(
            seq_count * block_tiles, WINDOW_LENGTH, heads_kv, query_group_width, HEAD_DIMENSION
        ),
    ] + block_facts(query_lines, key_lines, doc_starts, valid_counts, row_count)
    main_count = seq_count * block_tiles
    dq_all, dk_all, dv_all, sink_part = blockwise(entries, sinks)
    dk_main = dk_all.reshape(seq_count, block_tiles, 2 * WINDOW_LENGTH, kv_width)
    dv_main = dv_all.reshape(seq_count, block_tiles, 2 * WINDOW_LENGTH, kv_width)
    edge_keys, edge_values = (
        passed_along(dk_main[:, 0, :WINDOW_LENGTH].astype(jnp.bfloat16), "ctx", -1).astype(
            jnp.float32
        ),
        passed_along(dv_main[:, 0, :WINDOW_LENGTH].astype(jnp.bfloat16), "ctx", -1).astype(
            jnp.float32
        ),
    )
    key_total = dk_main[:, :, WINDOW_LENGTH:] + jnp.concatenate(
        [dk_main[:, 1:, :WINDOW_LENGTH], edge_keys[:, None]], axis=1
    )
    value_total = dv_main[:, :, WINDOW_LENGTH:] + jnp.concatenate(
        [dv_main[:, 1:, :WINDOW_LENGTH], edge_values[:, None]], axis=1
    )
    query_grad = dq_all.reshape(seq_count, row_count, query_width).astype(jnp.bfloat16)
    key_grad = key_total.reshape(seq_count, row_count, kv_width).astype(jnp.bfloat16)
    value_grad = value_total.reshape(seq_count, row_count, kv_width).astype(jnp.bfloat16)
    sink_grad = lax.psum(jnp.sum(sink_part, axis=0), ("dp", "ctx"))
    return (query_grad, key_grad, value_grad, sink_grad)


def solution(mesh):
    placed = (
        P("dp", "ctx", "tp"),
        P("dp", "ctx", "tp"),
        P("dp", "ctx", "tp"),
        P("dp", "ctx", "tp"),
        P("tp"),
        P("dp", None),
        P("dp", None),
    )
    return jax.shard_map(
        local,
        mesh=mesh,
        in_specs=placed,
        out_specs=(P("dp", "ctx", "tp"), P("dp", "ctx", "tp"), P("dp", "ctx", "tp"), P("tp")),
        check_vma=False,
    )
```

profile of v0, /device:TPU:0, one launch (start us, length us, event | category | flops | bytes accessed | tf_op | source)
XLA Modules:
  0.0 94.8 jit_solution(16104393274618011304)
XLA Ops:
  0.6 4.9 %collective-permute-start = (bf16[2,128,256]{2,1,0:T(8,128)(2,1)}, bf16[2,128,256]{2,1,0:T(8,128)(2,1)S(1)}, u32[]{:S(2)}, u32[]{:S(2)}) collective-permute-start(bf16[2,128,256]{2,1,0:T(8,128)(2,1)} %param.8), channel_id=1, source_target_pairs={{0,2},{2,4},{4,6},{6,8},{8,10},{10,12},{12,14},{1,3},{3,5},{5,7},{... | collective-permute-start | bytes 393224 | tf_op jit(solution)/shard_map/ppermute | solution.py:18
  5.5 4.1 %collective-permute-start.1 = (bf16[2,128,256]{2,1,0:T(8,128)(2,1)}, bf16[2,128,256]{2,1,0:T(8,128)(2,1)}, u32[]{:S(2)}, u32[]{:S(2)}) collective-permute-start(bf16[2,128,256]{2,1,0:T(8,128)(2,1)} %param.9), channel_id=1, source_target_pairs={{0,2},{2,4},{4,6},{6,8},{8,10},{10,12},{12,14},{1,3},{3,5},{5,7},{... | collective-permute-start | bytes 393224 | tf_op jit(solution)/shard_map/ppermute | solution.py:18
  9.7 0.8 slice_bitcast_fusion
  10.4 0.1 select_reduce_fusion.1
  10.5 0.8 slice_bitcast_fusion.2
  11.3 0.1 convert_reduce_fusion.1
  11.4 0.1 convert_reduce_fusion.3
  11.5 1.6 %copy.43 = bf16[2,128,2048]{1,2,0:T(8,128)(2,1)S(1)} copy(bf16[2,128,2048]{2,1,0:T(8,128)(2,1)} %param.7) | data formatting | bytes 2097152 | tf_op args[0]
  13.1 0.7 max.21
  13.9 1.6 %copy.47 = bf16[2,128,2048]{1,2,0:T(8,128)(2,1)S(1)} copy(bf16[2,128,2048]{2,1,0:T(8,128)(2,1)} %param.10) | data formatting | bytes 2097152 | tf_op args[3]
  15.6 0.3 fusion.17
  15.8 0.9 pad_maximum_fusion
  16.8 0.2 reshape.371
  17.0 0.2 fusion.29
  17.2 0.2 copy.69
  17.4 0.2 copy.70
  17.5 0.0 copy-start.5
  17.5 1.3 %fusion.4 = (f32[2,4,8,128]{3,2,1,0:T(8,128)S(1)}, f32[2,4,256,128,8]{3,2,4,1,0:T(8,128)S(1)}) fusion(pred[2,128,256]{1,2,0:T(8,128)(4,1)S(1)} %fusion.17, bf16[2,128,4,8,64]{1,4,3,2,0:T(8,128)(2,1)S(1)} %bitcast.104, bf16[2,1,128,4,64]{2,4,3,0,1:T(8,128)(2,1)S(1)} %copy.70, bf16[2,1,128,4,64]{2,4,3,0,1:T(8,128)(2,1)S(1)} %copy.69), kind=kOutput, calls=%fused_computation.7 | convolution fusion | flops 275243008 | bytes 9797632 | tf_op jit(solution)/shard_map/while/body/eval_jaxpr/nqhgd,nkhd->nhgqk/dot_general | solution.py:49
  18.9 0.1 broadcast_maximum_fusion
  18.9 3.1 %copy-done = f32[2,4,256,128,8]{3,2,4,1,0:T(8,128)} copy-done((f32[2,4,256,128,8]{3,2,4,1,0:T(8,128)}, f32[2,4,256,128,8]{3,2,4,1,0:T(8,128)S(1)}, u32[]{:S(2)}) %copy-start) | copy-done | bytes 8388632
  22.1 2.3 %fusion.3 = f32[2,4,8,128]{3,2,1,0:T(8,128)S(1)} fusion(f32[2,4,256,128,8]{3,2,4,1,0:T(8,128)S(1)} %get-tuple-element.80, f32[2,4,8,128]{3,2,1,0:T(8,128)S(1)} %broadcast_maximum_fusion, pred[2,128,256]{1,2,0:T(8,128)(4,1)S(1)} %fusion.17), kind=kLoop, calls=%fused_computation.6 | loop fusion | flops 8380416 | bytes 8519680 | tf_op jit(solution)/shard_map/while/body/eval_jaxpr/reduce_sum | solution.py:66
  24.3 0.7 fusion.21
  25.0 0.9 pad_maximum_fusion.1
  26.0 0.2 reshape.372
  26.2 0.2 fusion.30
  26.4 0.2 copy.71
  26.6 0.2 copy.72
  26.8 0.0 copy-start.6
  26.8 4.7 %fusion.6 = f32[2,4,256,64,1]{2,3,4,1,0:T(8,128)S(1)} fusion(bf16[2,128,4,8,64]{1,4,3,2,0:T(8,128)(2,1)S(1)} %bitcast.109, f32[2,4,256,128,8]{3,2,4,1,0:T(8,128)} %copy-done, f32[2,4,8,128]{3,2,1,0:T(8,128)} %fusion.21, f32[2,4,8,128]{3,2,1,0:T(8,128)} %copy-done.3, pred[2,128,256]{1,2,0:T(8,128)(4,1)S(1)} %fusion.17), kind=kOutput, calls=%fused_computation.11 | convolution fusion | flops 278921216 | bytes 10092544 | tf_op jit(solution)/shard_map/while/body/eval_jaxpr/nhgqk,nqhgd->nkhd/dot_general | solution.py:92
  31.4 0.0 copy-start.1
  31.5 0.8 copy.76
  32.3 1.7 %collective-permute-start.3 = (bf16[2,128,256]{2,1,0:T(8,128)(2,1)}, bf16[2,128,256]{2,1,0:T(8,128)(2,1)S(1)}, u32[]{:S(2)}, u32[]{:S(2)}) collective-permute-start(bf16[2,128,256]{2,1,0:T(8,128)(2,1)} %bitcast.114), channel_id=1, source_target_pairs={{2,0},{4,2},{6,4},{8,6},{10,8},{12,10},{14,12},{3,1},{5,3},{7,5},{... | collective-permute-start | bytes 393224 | tf_op jit(solution)/shard_map/ppermute | solution.py:18
  34.0 6.4 %fusion.5 = f32[2,4,8,128]{3,2,1,0:T(8,128)S(1)} fusion(bf16[2,128,4,8,64]{1,4,3,2,0:T(8,128)(2,1)S(1)} %bitcast.110, bf16[2,1,128,4,64]{2,4,3,0,1:T(8,128)(2,1)S(1)} %copy.72, bf16[2,1,128,4,64]{2,4,3,0,1:T(8,128)(2,1)S(1)} %copy.71, f32[2,4,256,128,8]{3,2,4,1,0:T(8,128)} %copy-done, f32[2,4,8,128]{3,2,1,0:T(8,128)S(1)} %copy-done.6, ...), kind=kOutput, calls=%fused_computation.9 | convolution fusion | flops 281010176 | bytes 9863168 | tf_op jit(solution)/shard_map/while/body/eval_jaxpr/nhgqk,nkhd->nhgqd/dot_general | solution.py:69
  40.5 3.0 %fusion.1 = bf16[2,4,8,128,256]{3,4,2,1,0:T(8,128)(2,1)S(1)} fusion(f32[2,4,8,128]{3,2,1,0:T(8,128)S(1)} %fusion.5, bf16[2,128,4,8,64]{1,4,3,2,0:T(8,128)(2,1)S(1)} %bitcast.111, bf16[2,1,128,4,64]{2,4,3,0,1:T(8,128)(2,1)S(1)} %copy.72, bf16[2,1,128,4,64]{2,4,3,0,1:T(8,128)(2,1)S(1)} %copy.71, f32[2,4,8,128]{3,2,1,0:T(8,128)S(1)} %copy-done.6, ...), kind=kOutput, calls=%fused_computation.2 | convolution fusion | flops 283639808 | bytes 14057472 | tf_op jit(solution)/shard_map/while/body/eval_jaxpr/nqhgd,nkhd->nhgqk/dot_general | solution.py:75
  43.5 0.0 copy-start.2
  43.5 1.4 %fusion.10 = f32[2,4,256,64]{2,3,1,0:T(8,128)S(1)} fusion(bf16[2,4,8,128,256]{3,4,2,1,0:T(8,128)(2,1)S(1)} %fusion.1, bf16[2,128,4,8,64]{1,4,3,2,0:T(8,128)(2,1)S(1)} %bitcast.105), kind=kOutput, calls=%fused_computation.16 | convolution fusion | flops 268566528 | bytes 5767168 | tf_op jit(solution)/shard_map/while/body/eval_jaxpr/nhgqk,nqhgd->nkhd/dot_general | solution.py:87
  44.9 0.8 multiply_convert_fusion
  45.8 0.2 multiply_reduce_fusion
  46.0 0.1 neg.9
  46.1 0.1 copy.75
  46.2 0.1 copy.73
  46.3 0.1 copy.74
  46.5 1.3 %collective-permute-start.2 = (bf16[2,128,256]{2,1,0:T(8,128)(2,1)S(1)}, bf16[2,128,256]{2,1,0:T(8,128)(2,1)S(1)}, u32[]{:S(2)}, u32[]{:S(2)}) collective-permute-start(bf16[2,128,256]{2,1,0:T(8,128)(2,1)S(1)} %bitcast.115), channel_id=1, source_target_pairs={{2,0},{4,2},{6,4},{8,6},{10,8},{12,10},{14,12},{3,1},{5,3},{7,5},{... | collective-permute-start | bytes 393224 | tf_op jit(solution)/shard_map/ppermute | solution.py:18
  47.8 1.3 %copy.56 = bf16[2,128,2048]{2,1,0:T(8,128)(2,1)} copy(bf16[2,128,2048]{1,2,0:T(8,128)(2,1)S(1)} %bitcast.106) | data formatting | bytes 2097152
  49.1 44.4 %psum.7 = f32[32]{0:T(128)} all-reduce(f32[32]{0:T(128)S(1)} %neg.9), channel_id=1, replica_groups=mesh['dp'=2,'ctx'=8,'tp'=2] {'dp','ctx'}, use_global_device_ids=true, to_apply=%region_10.11 | all-reduce | flops 32 | bytes 256 | tf_op jit(solution)/shard_map/psum | solution.py:194
  93.4 0.7 fusion.20
  94.1 0.0 collective-permute-done.2
  94.1 0.7 fusion.19
  (33 shorter events, 0.2 us)
Async XLA Ops:
  0.6 15.2 %collective-permute-start = (bf16[2,128,256]{2,1,0:T(8,128)(2,1)}, bf16[2,128,256]{2,1,0:T(8,128)(2,1)S(1)}, u32[]{:S(2)}, u32[]{:S(2)}) collective-permute-start(bf16[2,128,256]{2,1,0:T(8,128)(2,1)} %param.8), channel_id=1, source_target_pairs={{0,2},{2,4},{4,6},{6,8},{8,10},{10,12},{12,14},{1,3},{3,5},{5,7},{... | collective-permute-start | bytes 393224 | tf_op jit(solution)/shard_map/ppermute | solution.py:18
  5.5 19.5 %collective-permute-start.1 = (bf16[2,128,256]{2,1,0:T(8,128)(2,1)}, bf16[2,128,256]{2,1,0:T(8,128)(2,1)}, u32[]{:S(2)}, u32[]{:S(2)}) collective-permute-start(bf16[2,128,256]{2,1,0:T(8,128)(2,1)} %param.9), channel_id=1, source_target_pairs={{0,2},{2,4},{4,6},{6,8},{8,10},{10,12},{12,14},{1,3},{3,5},{5,7},{... | collective-permute-start | bytes 393224 | tf_op jit(solution)/shard_map/ppermute | solution.py:18
  17.5 7.5 %copy-start.5 = (bf16[2,128,256]{2,1,0:T(8,128)(2,1)S(1)}, bf16[2,128,256]{2,1,0:T(8,128)(2,1)}, u32[]{:S(2)}) copy-start(bf16[2,128,256]{2,1,0:T(8,128)(2,1)} %param.9) | copy-start | bytes 393220
  18.9 3.2 %copy-start = (f32[2,4,256,128,8]{3,2,4,1,0:T(8,128)}, f32[2,4,256,128,8]{3,2,4,1,0:T(8,128)S(1)}, u32[]{:S(2)}) copy-start(f32[2,4,256,128,8]{3,2,4,1,0:T(8,128)S(1)} %get-tuple-element.80) | copy-start | bytes 25165828
  18.9 6.1 %copy-start.3 = (f32[2,4,8,128]{3,2,1,0:T(8,128)}, f32[2,4,8,128]{3,2,1,0:T(8,128)S(1)}, u32[]{:S(2)}) copy-start(f32[2,4,8,128]{3,2,1,0:T(8,128)S(1)} %broadcast_maximum_fusion) | copy-start | bytes 98308
  26.7 7.3 %copy-start.4 = (f32[2,4,8,128]{3,2,1,0:T(8,128)S(1)}, f32[2,4,8,128]{3,2,1,0:T(8,128)}, u32[]{:S(2)}) copy-start(f32[2,4,8,128]{3,2,1,0:T(8,128)} %copy-done.3) | copy-start | bytes 98308
  26.8 7.3 %copy-start.6 = (f32[2,4,8,128]{3,2,1,0:T(8,128)S(1)}, f32[2,4,8,128]{3,2,1,0:T(8,128)}, u32[]{:S(2)}) copy-start(f32[2,4,8,128]{3,2,1,0:T(8,128)} %fusion.21) | copy-start | bytes 98308
  31.4 9.0 %copy-start.1 = (f32[2,4,256,64,1]{2,3,4,1,0:T(8,128)}, f32[2,4,256,64,1]{2,3,4,1,0:T(8,128)S(1)}, u32[]{:S(2)}) copy-start(f32[2,4,256,64,1]{2,3,4,1,0:T(8,128)S(1)} %fusion.6) | copy-start | bytes 1572868
  32.3 8.2 %slice-start = ((s8[8388608]{0:T(1024)(128)(4,1)}), s8[4194304]{0:T(1024)(128)(4,1)S(1)}, s32[]{:S(2)}) async-start(s8[8388608]{0:T(1024)(128)(4,1)} %bitcast.102), calls=%async_computation | async-start | bytes 8388608
  32.3 8.2 %slice-start.1 = ((s8[8388608]{0:T(1024)(128)(4,1)}), s8[4194304]{0:T(1024)(128)(4,1)S(1)}, s32[]{:S(2)}) async-start(s8[8388608]{0:T(1024)(128)(4,1)} %bitcast.102), calls=%async_computation.1 | async-start | bytes 8388608
  32.3 61.2 %collective-permute-start.3 = (bf16[2,128,256]{2,1,0:T(8,128)(2,1)}, bf16[2,128,256]{2,1,0:T(8,128)(2,1)S(1)}, u32[]{:S(2)}, u32[]{:S(2)}) collective-permute-start(bf16[2,128,256]{2,1,0:T(8,128)(2,1)} %bitcast.114), channel_id=1, source_target_pairs={{2,0},{4,2},{6,4},{8,6},{10,8},{12,10},{14,12},{3,1},{5,3},{7,5},{... | collective-permute-start | bytes 393224 | tf_op jit(solution)/shard_map/ppermute | solution.py:18
  43.5 2.2 %copy-start.2 = (f32[2,4,256,64,1]{2,3,4,1,0:T(8,128)S(1)}, f32[2,4,256,64,1]{2,3,4,1,0:T(8,128)}, u32[]{:S(2)}) copy-start(f32[2,4,256,64,1]{2,3,4,1,0:T(8,128)} %copy-done.1) | copy-start | bytes 1572868
  46.5 47.7 %collective-permute-start.2 = (bf16[2,128,256]{2,1,0:T(8,128)(2,1)S(1)}, bf16[2,128,256]{2,1,0:T(8,128)(2,1)S(1)}, u32[]{:S(2)}, u32[]{:S(2)}) collective-permute-start(bf16[2,128,256]{2,1,0:T(8,128)(2,1)S(1)} %bitcast.115), channel_id=1, source_target_pairs={{2,0},{4,2},{6,4},{8,6},{10,8},{12,10},{14,12},{3,1},{5,3},{7,5},{... | collective-permute-start | bytes 393224 | tf_op jit(solution)/shard_map/ppermute | solution.py:18
where the time goes:
time: 95.1 us; the launch traced here: 94.8 us
  blocking collectives  44.4 us (47%)
  matrix products  17.6 us (19%)
  local copies, waits for them, and re-layouts  12.8 us (13%)
  starting transfers between devices  12 us (13%)
  other arithmetic  7.06 us (7%)
  between operations  1.01 us (1%)
    psum x1, blocking collectives, local(): sink_grad = lax.psum(jnp.sum(sink_part, axis=0), ('dp', 'ctx'))  44.4 us
    ppermute x4, starting transfers between devices, passed_along(): lax.ppermute(value, axis, [(source, source + steps) for source in range(f...  12 us
    unnamed x29, local copies, waits for them, and re-layouts  9.51 us
    dot_general x1, matrix products, band_grads(): jnp.einsum('nhgqk,nkhd->nhgqd', attend_low, value_tile_block, preferred_e...  6.43 us
    dot_general x1, matrix products, band_grads(): jnp.einsum('nhgqk,nqhgd->nkhd', attend_low, output_grad_block, preferred_...  4.66 us
    dot_general x1, matrix products, band_grads(): jnp.einsum('nqhgd,nkhd->nhgqk', output_grad_block, value_tile_block, pref...  3 us
    reduce_sum x1, other arithmetic, band_grads(): denominator = jnp.sum(powers, axis=-1) + sink_exp  2.26 us
  transfers between devices with their start and end apart: 4, of which 0 were waited for; matrix products, arithmetic and copies ran while one was open for 28% of the time, Pallas kernels for 0%

commit v1 on v0

v1 whole, which is shorter than its diff:
```python
import functools

import jax
import jax.numpy as jnp
from jax import lax
from jax.experimental import pallas as pl
from jax.experimental.pallas import tpu as pltpu
from jax.sharding import PartitionSpec as P

HEAD = 64
WINDOW = 128
LANES = 128
HALF = WINDOW // 2
SPAN = WINDOW + HALF
masked_score = -1e30
MESH = pl.DeviceIdType.MESH
F32 = jnp.float32
BF16 = jnp.bfloat16

NT_DIMS = (((1,), (1,)), ((), ()))


def mm(a, b):
    return jnp.dot(a, b, preferred_element_type=F32)


def mm_nt(a, b):
    return lax.dot_general(a, b, NT_DIMS, preferred_element_type=F32)


def kernel(
    n_dp, n_ctx, seqs, pairs,
    q_ref, k_ref, v_ref, g_ref, sinks_ref, starts_ref, counts_ref,
    dq_ref, dk_ref, dv_ref, sg_ref,
    qbuf, gbuf, kvown, kvhalo, dqbuf, bias, gsend, grecv, gown, sacc, ssend, srecv,
    in_sem, out_sem, hs_sem, hr_sem, gs_sem, gr_sem, ss_sem, sr_sem,
):
    dp, ctx, tp = lax.axis_index("dp"), lax.axis_index("ctx"), lax.axis_index("tp")
    chunks = seqs * pairs
    group = n_dp * n_ctx
    me = dp * n_ctx + ctx
    qw = q_ref.shape[2] // pairs
    docs = starts_ref.shape[1]
    n_sinks = sinks_ref.shape[0]
    scale = HEAD ** -0.5

    def peer(i):
        other = lax.rem(me + i, group)
        return (other // n_ctx, lax.rem(other, n_ctx), tp)

    barrier = pltpu.get_barrier_semaphore()

    def greet(i, carry):
        pl.semaphore_signal(barrier, inc=1, device_id=peer(i), device_id_type=MESH)
        return carry

    lax.fori_loop(1, group, greet, 0)

    def local_copies(t):
        b, cp = t // pairs, lax.rem(t, pairs)
        wide = pl.ds(pl.multiple_of(cp * qw, LANES), qw)
        thin = pl.ds(pl.multiple_of(cp * LANES, LANES), LANES)
        return (
            pltpu.make_async_copy(k_ref.at[b, :, thin], kvown.at[0, t], in_sem.at[0, t]),
            pltpu.make_async_copy(v_ref.at[b, :, thin], kvown.at[1, t], in_sem.at[1, t]),
            pltpu.make_async_copy(q_ref.at[b, :, wide], qbuf.at[t], in_sem.at[2, t]),
            pltpu.make_async_copy(g_ref.at[b, :, wide], gbuf.at[t], in_sem.at[3, t]),
        )

    for t in range(chunks):
        for copy in local_copies(t):
            copy.start()

    def out_copy(t):
        b, cp = t // pairs, lax.rem(t, pairs)
        wide = pl.ds(pl.multiple_of(cp * qw, LANES), qw)
        return pltpu.make_async_copy(dqbuf.at[t], dq_ref.at[b, :, wide], out_sem.at[t])

    def halo_copies(t):
        b, cp = t // pairs, lax.rem(t, pairs)
        thin = pl.ds(pl.multiple_of(cp * LANES, LANES), LANES)
        target = (dp, lax.rem(ctx + 1, n_ctx), tp)
        return tuple(
            pltpu.make_async_remote_copy(
                src_ref=ref.at[b, :, thin], dst_ref=kvhalo.at[w, t],
                send_sem=hs_sem.at[w, t], recv_sem=hr_sem.at[w, t],
                device_id=target, device_id_type=MESH,
            )
            for w, ref in enumerate((k_ref, v_ref))
        )

    def grad_copies(t):
        target = (dp, lax.rem(ctx + n_ctx - 1, n_ctx), tp)
        return tuple(
            pltpu.make_async_remote_copy(
                src_ref=gsend.at[w, t], dst_ref=grecv.at[w, t],
                send_sem=gs_sem.at[w, t], recv_sem=gr_sem.at[w, t],
                device_id=target, device_id_type=MESH,
            )
            for w in range(2)
        )

    def sink_copy(i):
        return pltpu.make_async_remote_copy(
            src_ref=ssend, dst_ref=srecv.at[i - 1],
            send_sem=ss_sem.at[i - 1], recv_sem=sr_sem.at[i - 1],
            device_id=peer(i), device_id_type=MESH,
        )

    lane = lax.broadcasted_iota(jnp.int32, (1, LANES), 1)
    low_lane = lane < HEAD
    start = ctx * WINDOW
    for b in range(seqs):
        fold = lax.rem(lane, HALF)
        pos_parts = [start + fold, start + HALF + fold, start - WINDOW + lane, start + lane]
        ids = [jnp.zeros((1, LANES), F32) for _ in pos_parts]
        for d in range(docs):
            s = starts_ref[b, d]
            ids = [x + (s <= pos).astype(F32) for x, pos in zip(ids, pos_parts)]
        key_doc = jnp.concatenate(
            [jnp.transpose(jnp.broadcast_to(x, (LANES, LANES))) for x in ids[2:]], axis=0
        )
        krow = lax.broadcasted_iota(jnp.int32, (2 * WINDOW, LANES), 0)
        kpos = krow - WINDOW
        prev_limit = counts_ref[b, lax.rem(ctx + n_ctx - 1, n_ctx)]
        own_limit = counts_ref[b, ctx]
        first = (ctx == 0).astype(jnp.int32)
        limit = jnp.where(krow < WINDOW, prev_limit * (1 - first), own_limit + WINDOW)
        valid = krow < limit
        for h in range(2):
            qpos = jnp.broadcast_to(h * HALF + fold, (2 * WINDOW, LANES))
            ok = (kpos <= qpos) & (qpos - kpos < WINDOW) & valid & (key_doc == ids[h])
            whole = jnp.where(ok, 0.0, masked_score).astype(F32)
            bias[b, h] = whole[h * HALF : h * HALF + SPAN]

    sacc[...] = jnp.zeros_like(sacc)

    pl.semaphore_wait(barrier, group - 1)

    @pl.when(ctx < n_ctx - 1)
    def _():
        for t in range(chunks):
            for copy in halo_copies(t):
                copy.start()

    @pl.when(ctx == 0)
    def _():
        kvhalo[...] = jnp.zeros_like(kvhalo)

    keep0 = low_lane.astype(F32).astype(BF16)
    keep1 = (1.0 - low_lane.astype(F32)).astype(BF16)

    def spread(tile, ci):
        wide = tile.astype(F32)
        turned = pltpu.roll(wide, HEAD, 1)
        return jnp.where(low_lane, wide, turned) if ci == 0 else jnp.where(low_lane, turned, wide)

    def step(t, carry):
        b, cp = t // pairs, lax.rem(t, pairs)
        for copy in local_copies(t):
            copy.wait()

        @pl.when(ctx > 0)
        def _():
            for copy in halo_copies(t):
                copy.wait_recv()

        kpair = jnp.concatenate([kvhalo[0, t], kvown[0, t]], axis=0)
        vpair = jnp.concatenate([kvhalo[1, t], kvown[1, t]], axis=0)
        sums = []
        for ci in range(2):
            kwide = spread(kpair, ci) * scale
            k2 = kwide.astype(BF16)
            v2 = spread(vpair, ci).astype(BF16)
            dk_parts, dv_parts = [], []
            for h in range(2):
                r0 = h * HALF
                kcut, vcut = k2[r0 : r0 + SPAN], v2[r0 : r0 + SPAN]
                turned = kwide if h == 0 else jnp.concatenate([kwide[HALF:], kwide[:HALF]], axis=0)
                kt = jnp.transpose(turned)[:HEAD, :SPAN].astype(BF16)
                band = bias[b, h]
                band = jnp.concatenate([band, band], axis=1)
                wq_all, wg_all, p_all, d_all = [], [], [], []
                for quad in range(2):
                    base = ci * (qw // 2) + quad * 2 * LANES
                    qs = [qbuf[t, r0 : r0 + HALF, base + p * LANES : base + (p + 1) * LANES] for p in range(2)]
                    gs = [gbuf[t, r0 : r0 + HALF, base + p * LANES : base + (p + 1) * LANES] for p in range(2)]
                    wq = jnp.concatenate([x * keep for keep in (keep0, keep1) for x in qs], axis=0)
                    wg = jnp.concatenate([x * keep for keep in (keep0, keep1) for x in gs], axis=0)
                    head0 = (cp * 2 + ci) * (n_sinks // (2 * pairs)) + quad * 4
                    sink = jnp.concatenate(
                        [
                            jnp.where(low_lane, sinks_ref[head0 + e], sinks_ref[head0 + 2 + e])
                            for e in range(2)
                        ],
                        axis=1,
                    )
                    scores = mm_nt(kcut, wq) + band
                    top = jnp.maximum(jnp.max(scores, axis=0, keepdims=True), sink)
                    powers = jnp.exp(scores - top)
                    sink_exp = jnp.exp(sink - top)
                    inv = 1.0 / (jnp.sum(powers, axis=0, keepdims=True) + sink_exp)
                    prob = powers * inv
                    dprob = mm_nt(vcut, wg)
                    delta = jnp.sum(prob * dprob, axis=0, keepdims=True)
                    dscore = (prob * (dprob - delta)).astype(BF16)
                    dqt = mm(kt, dscore)
                    dq2 = jnp.transpose(jnp.concatenate([dqt[:, :LANES], dqt[:, LANES:]], axis=0)).astype(BF16)
                    for p in range(2):
                        dqbuf[t, r0 : r0 + HALF, base + p * LANES : base + (p + 1) * LANES] = dq2[
                            p * HALF : (p + 1) * HALF
                        ]
                    row = ci * 2 + quad
                    sacc[cp, row : row + 1, :] -= sink_exp * inv * delta
                    wq_all.append(wq)
                    wg_all.append(wg)
                    p_all.append(prob.astype(BF16))
                    d_all.append(dscore)
                dv_parts.append(mm(jnp.concatenate(p_all, axis=1), jnp.concatenate(wg_all, axis=0)))
                dk_parts.append(mm(jnp.concatenate(d_all, axis=1), jnp.concatenate(wq_all, axis=0)))
            totals = []
            for lo, hi in (dk_parts, dv_parts):
                x = jnp.concatenate([lo[:HALF], lo[HALF:] + hi[:WINDOW], hi[WINDOW:]], axis=0)
                totals.append(x + pltpu.roll(x, HEAD, 1))
            sums.append(totals)
        for w in range(2):
            x = jnp.where(low_lane, sums[0][w], sums[1][w])
            if w == 0:
                x = x * scale
            gsend[w, t] = x[:WINDOW].astype(BF16)
            gown[w, t] = x[WINDOW:]

        @pl.when(ctx > 0)
        def _():
            for copy in grad_copies(t):
                copy.start()

        out_copy(t).start()
        return carry

    lax.fori_loop(0, chunks, step, 0)

    lane4 = lax.broadcasted_iota(jnp.int32, (4, LANES), 1)
    row4 = lax.broadcasted_iota(jnp.int32, (4, LANES), 0)
    mine = jnp.zeros((1, LANES), F32)
    for cp in range(pairs):
        part = sacc[cp]
        for e in range(2):
            cut = part[:, e * LANES : (e + 1) * LANES]
            for p in range(2):
                chosen = low_lane if p == 0 else jnp.logical_not(low_lane)
                seg = jnp.sum(jnp.where(chosen, cut, 0.0), axis=1, keepdims=True)
                spot = lane4 == cp * 16 + row4 * 4 + p * 2 + e
                mine = mine + jnp.sum(jnp.where(spot, seg, 0.0), axis=0, keepdims=True)
    ssend[...] = jnp.broadcast_to(mine, ssend.shape)

    def send_sink(i, carry):
        sink_copy(i).start()
        return carry

    lax.fori_loop(1, group, send_sink, 0)

    for t in range(chunks):
        b, cp = t // pairs, t % pairs
        cut = slice(cp * LANES, (cp + 1) * LANES)

        @pl.when(ctx < n_ctx - 1)
        def _():
            for copy in grad_copies(t):
                copy.wait_recv()
            for w, ref in enumerate((dk_ref, dv_ref)):
                ref[b, :, cut] = (gown[w, t] + grecv[w, t].astype(F32)).astype(BF16)

        @pl.when(ctx == n_ctx - 1)
        def _():
            for w, ref in enumerate((dk_ref, dv_ref)):
                ref[b, :, cut] = gown[w, t].astype(BF16)

    @pl.when(ctx < n_ctx - 1)
    def _():
        for t in range(chunks):
            for copy in halo_copies(t):
                copy.wait_send()

    @pl.when(ctx > 0)
    def _():
        for t in range(chunks):
            for copy in grad_copies(t):
                copy.wait_send()

    for t in range(chunks):
        out_copy(t).wait()

    def take_sink(i, total):
        sink_copy(i).wait()
        return total + srecv[i - 1]

    total = lax.fori_loop(1, group, take_sink, ssend[...])
    sg_ref[...] = total[:1, : sg_ref.shape[1]]


def local(n_dp, n_ctx, queries, keys, values, output_gradient, sinks, doc_starts, valid_counts):
    seqs, rows, query_width = queries.shape
    kv_width = keys.shape[2]
    assert rows == WINDOW and kv_width % LANES == 0
    pairs = kv_width // LANES
    assert query_width == kv_width * 8
    chunks = seqs * pairs
    group = n_dp * n_ctx
    any_spec = pl.BlockSpec(memory_space=pl.ANY)
    smem = pl.BlockSpec(memory_space=pltpu.SMEM)
    vmem = pl.BlockSpec(memory_space=pltpu.VMEM)
    wide = query_width // pairs
    dq, dk, dv, sg = pl.pallas_call(
        functools.partial(kernel, n_dp, n_ctx, seqs, pairs),
        out_shape=(
            jax.ShapeDtypeStruct(queries.shape, BF16),
            jax.ShapeDtypeStruct(keys.shape, BF16),
            jax.ShapeDtypeStruct(values.shape, BF16),
            jax.ShapeDtypeStruct((1, sinks.shape[0]), F32),
        ),
        in_specs=[any_spec] * 4 + [smem] * 3,
        out_specs=(any_spec, vmem, vmem, vmem),
        scratch_shapes=[
            pltpu.VMEM((chunks, rows, wide), BF16),
            pltpu.VMEM((chunks, rows, wide), BF16),
            pltpu.VMEM((2, chunks, rows, LANES), BF16),
            pltpu.VMEM((2, chunks, rows, LANES), BF16),
            pltpu.VMEM((chunks, rows, wide), BF16),
            pltpu.VMEM((seqs, 2, SPAN, LANES), F32),
            pltpu.VMEM((2, chunks, rows, LANES), BF16),
            pltpu.VMEM((2, chunks, rows, LANES), BF16),
            pltpu.VMEM((2, chunks, rows, LANES), F32),
            pltpu.VMEM((pairs, 4, 2 * LANES), F32),
            pltpu.VMEM((8, LANES), F32),
            pltpu.VMEM((group - 1, 8, LANES), F32),
            pltpu.SemaphoreType.DMA((4, chunks)),
            pltpu.SemaphoreType.DMA((chunks,)),
            pltpu.SemaphoreType.DMA((2, chunks)),
            pltpu.SemaphoreType.DMA((2, chunks)),
            pltpu.SemaphoreType.DMA((2, chunks)),
            pltpu.SemaphoreType.DMA((2, chunks)),
            pltpu.SemaphoreType.DMA((group - 1,)),
            pltpu.SemaphoreType.DMA((group - 1,)),
        ],
        compiler_params=pltpu.CompilerParams(
            collective_id=0, has_side_effects=True, vmem_limit_bytes=48 * 1024 * 1024
        ),
    )(queries, keys, values, output_gradient, sinks, doc_starts, valid_counts)
    return dq, dk, dv, sg.reshape(sinks.shape)


def solution(mesh):
    placed = (
        P("dp", "ctx", "tp"),
        P("dp", "ctx", "tp"),
        P("dp", "ctx", "tp"),
        P("dp", "ctx", "tp"),
        P("tp"),
        P("dp", None),
        P("dp", None),
    )
    return jax.shard_map(
        functools.partial(local, mesh.shape["dp"], mesh.shape["ctx"]),
        mesh=mesh,
        in_specs=placed,
        out_specs=(P("dp", "ctx", "tp"), P("dp", "ctx", "tp"), P("dp", "ctx", "tp"), P("tp")),
        check_vma=False,
    )
```

time: 95.1 us -> 38.3 us (0.40)
  blocking collectives: 44.4 us -> 0 us
  Pallas kernels: 0 us -> 28.4 us
  matrix products: 17.6 us -> 0 us
  starting transfers between devices: 12 us -> 0 us
  other arithmetic: 7.06 us -> 0 us
  local copies, waits for them, and re-layouts: 12.8 us -> 9.05 us
    psum x1 -> x0, blocking collectives: 44.4 us -> none  [local(): sink_grad = lax.psum(jnp.sum(sink_part, axis=0), ('dp', 'ctx'))]
    pallas_call x0 -> x1, Pallas kernels: none -> 28.4 us  [local(): pl.pallas_call(functools.partial(kernel, n_dp, n_ctx, seqs, pairs), out_s...]
    dot_general x6 -> x0, matrix products: 17.6 us -> none  [the longest x1 6.43 us: band_grads(): jnp.einsum('nhgqk,nkhd->nhgqd', attend_low, value_tile_block, preferred_e...]
    ppermute x4 -> x0, starting transfers between devices: 12 us -> none  [passed_along(): lax.ppermute(value, axis, [(source, source + steps) for source in range(f...]
    reduce_sum x5 -> x0, other arithmetic: 2.72 us -> none  [the longest x1 2.26 us: band_grads(): denominator = jnp.sum(powers, axis=-1) + sink_exp]
    concatenate x6 -> x0, other arithmetic: 1.89 us -> none  [the longest x1 0.93 us: local(): jnp.concatenate([halo_tails[0], keys], axis=1)]
    convert_element_type x2 -> x0, other arithmetic: 1.36 us -> none  [the longest x1 0.68 us: local(): value_total.reshape(seq_count, row_count, kv_width).astype(jnp.bfloat16)]
    unnamed x29 -> x18, local copies, waits for them, and re-layouts: 9.51 us -> 9.05 us
  transfers between devices with their start and end apart: 4 -> 0, of which waited for: 0 -> 0; matrix products, arithmetic and copies ran while one was open for 28% -> 0% of each run, Pallas kernels for 0% -> 0%
where the time goes in v1:
time: 38.3 us; the launch traced here: 38.1 us
  Pallas kernels  28.4 us (74%)
  local copies, waits for them, and re-layouts  9.05 us (24%)
  between operations  0.66 us (2%)
    pallas_call x1, Pallas kernels, local(): pl.pallas_call(functools.partial(kernel, n_dp, n_ctx, seqs, pairs), out_s...  28.4 us
    unnamed x18, local copies, waits for them, and re-layouts  9.05 us

profile of v1, /device:TPU:0, one launch (start us, length us, event | category | flops | bytes accessed | tf_op | source)
XLA Modules:
  0.0 38.1 jit_solution(12417204646856742871)
XLA Ops:
  0.6 0.0 copy-start
  0.6 1.2 %copy-done = bf16[2,128,2048]{2,1,0:T(8,128)(2,1)S(1)} copy-done((bf16[2,128,2048]{2,1,0:T(8,128)(2,1)S(1)}, bf16[2,128,2048]{2,1,0:T(8,128)(2,1)}, u32[]{:S(2)}) %copy-start) | copy-done | bytes 1048600
  1.9 0.0 copy-start.1
  1.9 1.2 %copy-done.1 = bf16[2,128,2048]{2,1,0:T(8,128)(2,1)S(1)} copy-done((bf16[2,128,2048]{2,1,0:T(8,128)(2,1)S(1)}, bf16[2,128,2048]{2,1,0:T(8,128)(2,1)}, u32[]{:S(2)}) %copy-start.1) | copy-done | bytes 1048600
  3.1 0.0 copy-start.2
  3.1 0.9 %copy-done.2 = bf16[2,128,256]{2,1,0:T(8,128)(2,1)S(1)} copy-done((bf16[2,128,256]{2,1,0:T(8,128)(2,1)S(1)}, bf16[2,128,256]{2,1,0:T(8,128)(2,1)}, u32[]{:S(2)}) %copy-start.2) | copy-done | bytes 131096
  4.0 0.0 copy-start.3
  4.0 0.9 %copy-done.3 = bf16[2,128,256]{2,1,0:T(8,128)(2,1)S(1)} copy-done((bf16[2,128,256]{2,1,0:T(8,128)(2,1)S(1)}, bf16[2,128,256]{2,1,0:T(8,128)(2,1)}, u32[]{:S(2)}) %copy-start.3) | copy-done | bytes 131096
  4.9 0.0 copy-start.4
  4.9 0.7 %copy-done.4 = s32[2,64]{1,0:T(2,128)S(1)} copy-done((s32[2,64]{1,0:T(2,128)S(1)}, s32[2,64]{1,0:T(2,128)}, u32[]{:S(2)}) %copy-start.4) | copy-done | bytes 536
  5.6 0.0 copy-start.5
  5.6 0.7 %copy-done.5 = s32[2,8]{1,0:T(2,128)S(1)} copy-done((s32[2,8]{1,0:T(2,128)S(1)}, s32[2,8]{1,0:T(2,128)}, u32[]{:S(2)}) %copy-start.5) | copy-done | bytes 88
  6.3 0.0 copy-start.6
  6.3 0.7 %copy-done.6 = f32[32]{0:T(128)S(1)} copy-done((f32[32]{0:T(128)S(1)}, f32[32]{0:T(128)}, u32[]{:S(2)}) %copy-start.6) | copy-done | bytes 152
  6.9 28.4 %shard_map.102 = (bf16[2,128,2048]{2,1,0:T(8,128)(2,1)S(1)}, bf16[2,128,256]{2,1,0:T(8,128)(2,1)S(1)}, bf16[2,128,256]{2,1,0:T(8,128)(2,1)S(1)}, f32[1,32]{1,0:T(1,128)S(1)}) custom-call(bf16[2,128,2048]{2,1,0:T(8,128)(2,1)S(1)} %copy-done, bf16[2,128,256]{2,1,0:T(8,128)(2,1)S(1)} %copy-done.2, bf16[2,128,256]{2,1,0:T(8,128)(2,1)S(1)} %copy-done.3, ...), custom_call_target="tpu_custom_call" | custom-call | tf_op jit(solution)/shard_map/pallas_call | solution.py:314
  35.3 1.0 %copy.15 = bf16[2,128,2048]{2,1,0:T(8,128)(2,1)} copy(bf16[2,128,2048]{2,1,0:T(8,128)(2,1)S(1)} %get-tuple-element.16) | data formatting | bytes 2097152
  36.3 0.7 %copy.16 = bf16[2,128,256]{2,1,0:T(8,128)(2,1)} copy(bf16[2,128,256]{2,1,0:T(8,128)(2,1)S(1)} %get-tuple-element.17) | data formatting | bytes 262144
  36.9 0.7 %copy.17 = bf16[2,128,256]{2,1,0:T(8,128)(2,1)} copy(bf16[2,128,256]{2,1,0:T(8,128)(2,1)S(1)} %get-tuple-element.18) | data formatting | bytes 262144
  37.6 0.5 %copy.18 = f32[32]{0:T(128)} copy(f32[32]{0:T(128)S(1)} %bitcast.1) | data formatting | bytes 256
Async XLA Ops:
  0.6 1.2 %copy-start = (bf16[2,128,2048]{2,1,0:T(8,128)(2,1)S(1)}, bf16[2,128,2048]{2,1,0:T(8,128)(2,1)}, u32[]{:S(2)}) copy-start(bf16[2,128,2048]{2,1,0:T(8,128)(2,1)} %q_ref.1) | copy-start | bytes 3145732
  1.9 1.2 %copy-start.1 = (bf16[2,128,2048]{2,1,0:T(8,128)(2,1)S(1)}, bf16[2,128,2048]{2,1,0:T(8,128)(2,1)}, u32[]{:S(2)}) copy-start(bf16[2,128,2048]{2,1,0:T(8,128)(2,1)} %g_ref.1) | copy-start | bytes 3145732
  3.1 0.9 %copy-start.2 = (bf16[2,128,256]{2,1,0:T(8,128)(2,1)S(1)}, bf16[2,128,256]{2,1,0:T(8,128)(2,1)}, u32[]{:S(2)}) copy-start(bf16[2,128,256]{2,1,0:T(8,128)(2,1)} %k_ref.1) | copy-start | bytes 393220
  4.0 0.9 %copy-start.3 = (bf16[2,128,256]{2,1,0:T(8,128)(2,1)S(1)}, bf16[2,128,256]{2,1,0:T(8,128)(2,1)}, u32[]{:S(2)}) copy-start(bf16[2,128,256]{2,1,0:T(8,128)(2,1)} %v_ref.1) | copy-start | bytes 393220
  4.9 0.7 %copy-start.4 = (s32[2,64]{1,0:T(2,128)S(1)}, s32[2,64]{1,0:T(2,128)}, u32[]{:S(2)}) copy-start(s32[2,64]{1,0:T(2,128)} %starts_ref.1) | copy-start | bytes 1540
  5.6 0.7 %copy-start.5 = (s32[2,8]{1,0:T(2,128)S(1)}, s32[2,8]{1,0:T(2,128)}, u32[]{:S(2)}) copy-start(s32[2,8]{1,0:T(2,128)} %counts_ref.1) | copy-start | bytes 196
  6.3 0.7 %copy-start.6 = (f32[32]{0:T(128)S(1)}, f32[32]{0:T(128)}, u32[]{:S(2)}) copy-start(f32[32]{0:T(128)} %sinks_ref.1) | copy-start | bytes 388

commit v2 on v1

--- a/solution.py
+++ b/solution.py
@@ -30,10 +30,10 @@
 
 def kernel(
     n_dp, n_ctx, seqs, pairs,
-    q_ref, k_ref, v_ref, g_ref, sinks_ref, starts_ref, counts_ref,
+    q_ref, k_ref, v_ref, g_ref, sinks_in, starts_in, counts_in,
     dq_ref, dk_ref, dv_ref, sg_ref,
-    qbuf, gbuf, kvown, kvhalo, dqbuf, bias, gsend, grecv, gown, sacc, ssend, srecv,
-    in_sem, out_sem, hs_sem, hr_sem, gs_sem, gr_sem, ss_sem, sr_sem,
+    qbuf, gbuf, kvown, kvhalo, sinks_ref, starts_ref, counts_ref, bias, gsend, grecv, gown, sacc, ssend, srecv,
+    in_sem, small_sem, hs_sem, hr_sem, gs_sem, gr_sem, ss_sem, sr_sem,
 ):
     dp, ctx, tp = lax.axis_index("dp"), lax.axis_index("ctx"), lax.axis_index("tp")
     chunks = seqs * pairs
@@ -67,14 +67,19 @@
             pltpu.make_async_copy(g_ref.at[b, :, wide], gbuf.at[t], in_sem.at[3, t]),
         )
 
+    smalls = [
+        pltpu.make_async_copy(src, dst, small_sem.at[i])
+        for i, (src, dst) in enumerate(
+            ((sinks_in, sinks_ref), (starts_in, starts_ref), (counts_in, counts_ref))
+        )
+    ]
+    for copy in smalls:
+        copy.start()
     for t in range(chunks):
         for copy in local_copies(t):
             copy.start()
-
-    def out_copy(t):
-        b, cp = t // pairs, lax.rem(t, pairs)
-        wide = pl.ds(pl.multiple_of(cp * qw, LANES), qw)
-        return pltpu.make_async_copy(dqbuf.at[t], dq_ref.at[b, :, wide], out_sem.at[t])
+    for copy in smalls:
+        copy.wait()
 
     def halo_copies(t):
         b, cp = t // pairs, lax.rem(t, pairs)
@@ -207,9 +212,8 @@
                     dqt = mm(kt, dscore)
                     dq2 = jnp.transpose(jnp.concatenate([dqt[:, :LANES], dqt[:, LANES:]], axis=0)).astype(BF16)
                     for p in range(2):
-                        dqbuf[t, r0 : r0 + HALF, base + p * LANES : base + (p + 1) * LANES] = dq2[
-                            p * HALF : (p + 1) * HALF
-                        ]
+                        spot = pl.ds(pl.multiple_of(cp * qw + base + p * LANES, LANES), LANES)
+                        dq_ref[b, r0 : r0 + HALF, spot] = dq2[p * HALF : (p + 1) * HALF]
                     row = ci * 2 + quad
                     sacc[cp, row : row + 1, :] -= sink_exp * inv * delta
                     wq_all.append(wq)
@@ -235,7 +239,6 @@
             for copy in grad_copies(t):
                 copy.start()
 
-        out_copy(t).start()
         return carry
 
     lax.fori_loop(0, chunks, step, 0)
@@ -288,15 +291,21 @@
             for copy in grad_copies(t):
                 copy.wait_send()
 
-    for t in range(chunks):
-        out_copy(t).wait()
-
     def take_sink(i, total):
         sink_copy(i).wait()
         return total + srecv[i - 1]
 
     total = lax.fori_loop(1, group, take_sink, ssend[...])
     sg_ref[...] = total[:1, : sg_ref.shape[1]]
+
+
+def write_out(*refs):
+    sems = refs[-1]
+    copies = [pltpu.make_async_copy(refs[i], refs[4 + i], sems.at[i]) for i in range(4)]
+    for copy in copies:
+        copy.start()
+    for copy in copies:
+        copy.wait()
 
 
 def local(n_dp, n_ctx, queries, keys, values, output_gradient, sinks, doc_starts, valid_counts):
@@ -307,8 +316,7 @@
     assert query_width == kv_width * 8
     chunks = seqs * pairs
     group = n_dp * n_ctx
-    any_spec = pl.BlockSpec(memory_space=pl.ANY)
-    smem = pl.BlockSpec(memory_space=pltpu.SMEM)
+    hbm = pl.BlockSpec(memory_space=pltpu.HBM)
     vmem = pl.BlockSpec(memory_space=pltpu.VMEM)
     wide = query_width // pairs
     dq, dk, dv, sg = pl.pallas_call(
@@ -319,14 +327,16 @@
             jax.ShapeDtypeStruct(values.shape, BF16),
             jax.ShapeDtypeStruct((1, sinks.shape[0]), F32),
         ),
-        in_specs=[any_spec] * 4 + [smem] * 3,
-        out_specs=(any_spec, vmem, vmem, vmem),
+        in_specs=[hbm] * 7,
+        out_specs=(vmem, vmem, vmem, vmem),
         scratch_shapes=[
             pltpu.VMEM((chunks, rows, wide), BF16),
             pltpu.VMEM((chunks, rows, wide), BF16),
             pltpu.VMEM((2, chunks, rows, LANES), BF16),
             pltpu.VMEM((2, chunks, rows, LANES), BF16),
-            pltpu.VMEM((chunks, rows, wide), BF16),
+            pltpu.SMEM(sinks.shape, F32),
+            pltpu.SMEM(doc_starts.shape, jnp.int32),
+            pltpu.SMEM(valid_counts.shape, jnp.int32),
             pltpu.VMEM((seqs, 2, SPAN, LANES), F32),
             pltpu.VMEM((2, chunks, rows, LANES), BF16),
             pltpu.VMEM((2, chunks, rows, LANES), BF16),
@@ -335,7 +345,7 @@
             pltpu.VMEM((8, LANES), F32),
             pltpu.VMEM((group - 1, 8, LANES), F32),
             pltpu.SemaphoreType.DMA((4, chunks)),
-            pltpu.SemaphoreType.DMA((chunks,)),
+            pltpu.SemaphoreType.DMA((3,)),
             pltpu.SemaphoreType.DMA((2, chunks)),
             pltpu.SemaphoreType.DMA((2, chunks)),
             pltpu.SemaphoreType.DMA((2, chunks)),
@@ -344,9 +354,17 @@
             pltpu.SemaphoreType.DMA((group - 1,)),
         ],
         compiler_params=pltpu.CompilerParams(
-            collective_id=0, has_side_effects=True, vmem_limit_bytes=48 * 1024 * 1024
+            collective_id=0, has_side_effects=True, vmem_limit_bytes=67_043_328
         ),
     )(queries, keys, values, output_gradient, sinks, doc_starts, valid_counts)
+    results = (dq, dk, dv, sg)
+    dq, dk, dv, sg = pl.pallas_call(
+        write_out,
+        out_shape=tuple(jax.ShapeDtypeStruct(x.shape, x.dtype) for x in results),
+        in_specs=[vmem] * 4,
+        out_specs=(hbm,) * 4,
+        scratch_shapes=[pltpu.SemaphoreType.DMA((4,))],
+    )(*results)
     return dq, dk, dv, sg.reshape(sinks.shape)
 
 

time: 38.3 us -> 32.2 us (0.84)
  local copies, waits for them, and re-layouts: 9.05 us -> 0 us
  Pallas kernels: 28.4 us -> 31.4 us
    unnamed x18 -> x0, local copies, waits for them, and re-layouts: 9.05 us -> none
    pallas_call x0 -> x1, Pallas kernels: none -> 2.39 us  [local(): pl.pallas_call(write_out, out_shape=tuple((jax.ShapeDtypeStruct(x.shape,...]
    pallas_call x1, Pallas kernels: 28.4 us -> 29 us  [local(): pl.pallas_call(functools.partial(kernel, n_dp, n_ctx, seqs, pairs), out_s...]
where the time goes in v2:
time: 32.2 us; the launch traced here: 32.1 us
  Pallas kernels  31.4 us (98%)
  between operations  0.64 us (2%)
    pallas_call x1, Pallas kernels, local(): pl.pallas_call(functools.partial(kernel, n_dp, n_ctx, seqs, pairs), out_s...  29 us
    pallas_call x1, Pallas kernels, local(): pl.pallas_call(write_out, out_shape=tuple((jax.ShapeDtypeStruct(x.shape,...  2.39 us

profile of v2, /device:TPU:0, one launch (start us, length us, event | category | flops | bytes accessed | tf_op | source)
XLA Modules:
  0.0 32.1 jit_solution(2895028498757206812)
XLA Ops:
  0.6 29.0 %shard_map.102 = (bf16[2,128,2048]{2,1,0:T(8,128)(2,1)}, bf16[2,128,256]{2,1,0:T(8,128)(2,1)}, bf16[2,128,256]{2,1,0:T(8,128)(2,1)}, f32[1,32]{1,0:T(1,128)}) custom-call(bf16[2,128,2048]{2,1,0:T(8,128)(2,1)} %q_ref.1, bf16[2,128,256]{2,1,0:T(8,128)(2,1)} %k_ref.1, bf16[2,128,256]{2,1,0:T(8,128)(2,1)} %v_ref.1, bf16[2,128,2048]{2,1,0:T(8,128)(2,1)} %g_ref.1, ...), custom_call_target="tpu_custom_call" | custom-call | tf_op jit(solution)/shard_map/pallas_call | solution.py:322
  29.7 2.4 %shard_map.103 = (bf16[2,128,2048]{2,1,0:T(8,128)(2,1)}, bf16[2,128,256]{2,1,0:T(8,128)(2,1)}, bf16[2,128,256]{2,1,0:T(8,128)(2,1)}, f32[1,32]{1,0:T(1,128)}) custom-call(bf16[2,128,2048]{2,1,0:T(8,128)(2,1)} %get-tuple-element.12.refs_0_, bf16[2,128,256]{2,1,0:T(8,128)(2,1)} %get-tuple-element.13.refs_1_, bf16[2,128,256]{2,1,0:T(8,128)(2,1)} %get-tuple-element.14.refs_2_, ...), custom_call_target="tpu_custom_call" | custom-call | tf_op jit(solution)/shard_map/pallas_call | solution.py:361
